TPU v7x, 32 devices: a whole 2x2x4 slice. The times are simulated.
32 devices in a mesh: grp: 2 (over x), path: 8 (over z, y), amp: 2 (over core).
Axes of the slice: x: 2, y: 2, z: 4, core: 2. Of those that a mesh axis runs over, the one named last changes fastest.
Arguments:
- left_slabs: bfloat16 [256, 2, 16384], P(('grp', 'path'), None, 'amp'), parts along dimension 0, may hold values from -0.59765625 to 0.59765625
- right_slabs: bfloat16 [256, 2, 8192], P(('grp', 'path'), None, 'amp'), parts along dimension 0, may hold values from -0.59765625 to 0.59765625
- term_index: int32 [256], P(('grp', 'path')), parts along dimension 0, may hold values from 0 to 3
- left_terms: float32 [4, 2, 2, 2], replicated, may hold values from -4.2 to 4.2
- right_terms: float32 [4, 2, 2, 2], replicated, may hold values from -4.2 to 4.2
- left_gates: bfloat16 [2, 2, 128, 128], replicated, may hold values from -0.375 to 0.375
- right_gates: bfloat16 [2, 2, 128, 128], replicated, may hold values from -0.375 to 0.375
Outputs:
- amplitudes: bfloat16 [2, 32768, 8192], P(None, ('grp', 'path'), 'amp'), parts along dimension 1
There are 2 independent parts, one for each index of `grp`. A program takes and returns all parts, laid end to end along the dimension named above; an argument that names none is the same for every part. Nothing has to cross between parts.
All inputs are finite; a program needn't handle non-finite values.
Results may differ from a plain program's by a relative error of at most 0.0081.
Values may be sent and summed in bfloat16 or wider, within the bound.
No kernel may reach another device: no remote copies, remote signals or barrier semaphores. Data moves between devices by JAX's collectives and lax.ppermute only.
A program may use at most 128 MiB of HBM per device.

v0:
```python
import jax
import jax.numpy as jnp
from jax import lax
from jax.sharding import PartitionSpec as P


def cut_term(slab, term_mix):
    paths_here, _, length = slab.shape
    width = min(128, length)
    values = slab.astype(jnp.float32).reshape(paths_here, 2, length // width, width)
    identity = jnp.eye(width // 2, dtype=jnp.float32)

    def expand(part):
        return jnp.einsum("ab,nmj->najbm", identity, part).reshape(paths_here, width, width)

    real_kron = expand(term_mix[:, 0])
    imag_kron = expand(term_mix[:, 1])
    batch_dims = (((2,), (1,)), ((0,), (0,)))

    def times(rows, kron):
        return lax.dot_general(
            rows,
            kron,
            batch_dims,
            precision=lax.Precision.HIGHEST,
            preferred_element_type=jnp.float32,
        )

    real_rows = values[:, 0]
    imag_rows = values[:, 1]
    real_part = times(real_rows, real_kron) - times(imag_rows, imag_kron)
    imag_part = times(real_rows, imag_kron) + times(imag_rows, real_kron)
    return jnp.stack([real_part, imag_part], 1).reshape(paths_here, 2, length).astype(jnp.bfloat16)


def apply_low(slab, gate_mat):
    paths_here, _, length = slab.shape
    gate_width = gate_mat.shape[-1]
    real_rows = slab[:, 0].reshape(-1, gate_width)
    imag_rows = slab[:, 1].reshape(-1, gate_width)
    upper = jnp.concatenate([gate_mat[0].T, gate_mat[1].T], 1)
    lower = jnp.concatenate([-gate_mat[1].T, gate_mat[0].T], 1)
    right_matrix = jnp.concatenate([upper, lower], 0)
    product = jnp.dot(
        jnp.concatenate([real_rows, imag_rows], 1), right_matrix, preferred_element_type=jnp.float32
    )
    real_part = product[:, :gate_width].reshape(paths_here, length)
    imag_part = product[:, gate_width:].reshape(paths_here, length)
    return jnp.stack([real_part, imag_part], 1).astype(jnp.bfloat16)


def stack_matrix(gate_mat):
    upper = jnp.concatenate([gate_mat[0], -gate_mat[1]], 1)
    lower = jnp.concatenate([gate_mat[1], gate_mat[0]], 1)
    return jnp.concatenate([upper, lower], 0)


def gate_rows(matrix, data):
    batch = jnp.broadcast_to(matrix, (data.shape[0],) + matrix.shape)
    return lax.dot_general(
        batch, data, (((2,), (1,)), ((0,), (0,))), preferred_element_type=jnp.float32
    )


def right_high(moved, gate_mat):
    half_paths = moved.shape[0]
    gate_width = gate_mat.shape[-1]
    low_width = gate_width // 2
    data = moved.reshape(half_paths, gate_width, gate_width)
    blocks = gate_mat.reshape(2, low_width, 2, low_width, 2)
    rows_index = jnp.arange(gate_width, dtype=jnp.int32)[:, None]
    cols_index = jnp.arange(gate_width, dtype=jnp.int32)[None, :]
    same_slot = rows_index % low_width == cols_index % low_width
    total = jnp.zeros((half_paths, gate_width, gate_width), jnp.float32)
    for target in range(2):
        for source in range(2):
            select = (
                same_slot
                & (rows_index // low_width == source)
                & (cols_index // low_width == target)
            ).astype(jnp.bfloat16)
            placed = jnp.dot(
                data.reshape(-1, gate_width), select, preferred_element_type=jnp.float32
            )
            placed = placed.astype(jnp.bfloat16).reshape(half_paths, gate_width, gate_width)
            matrix = stack_matrix(blocks[:, :, target, :, source])
            total = total + gate_rows(matrix, placed)
    return total.astype(jnp.bfloat16).reshape(half_paths, 2, -1)


def contract(left_part, right_part):
    left_stack = jnp.concatenate([left_part[:, 0], left_part[:, 1]], 0)
    right_real = jnp.concatenate([right_part[:, 0], -right_part[:, 1]], 0)
    right_imag = jnp.concatenate([right_part[:, 1], right_part[:, 0]], 0)
    contract_dims = (((0,), (0,)), ((), ()))
    real_part = lax.dot_general(
        left_stack, right_real, contract_dims, preferred_element_type=jnp.float32
    )
    imag_part = lax.dot_general(
        left_stack, right_imag, contract_dims, preferred_element_type=jnp.float32
    )
    return (real_part, imag_part)


def mixes(term_index, terms):
    chosen = (term_index[:, None] == jnp.arange(terms.shape[0], dtype=jnp.int32)[None, :]).astype(
        jnp.float32
    )
    flat = jnp.dot(chosen, terms.reshape(terms.shape[0], 8), precision=lax.Precision.HIGHEST)
    return flat.reshape(-1, 2, 2, 2)


def shards(left_slabs, right_slabs, term_index, left_terms, right_terms, left_gates, right_gates):
    gate_width = left_gates.shape[-1]
    path_count = lax.axis_size("path")
    left = cut_term(left_slabs, mixes(term_index, left_terms))
    left = apply_low(left, left_gates[0])
    moved = lax.all_to_all(left, "amp", split_axis=0, concat_axis=2, tiled=True)
    half_paths = moved.shape[0]
    full_left = moved.shape[2]
    turned = gate_rows(
        stack_matrix(left_gates[1]),
        moved.reshape(half_paths, 2 * gate_width, full_left // gate_width),
    )
    turned = turned.astype(jnp.bfloat16).reshape(half_paths, 2, full_left)
    portion = lax.all_to_all(turned, "path", split_axis=2, concat_axis=0, tiled=True)
    rows_here = portion.shape[2]
    portion = portion.reshape(path_count, half_paths, 2, rows_here)
    row_block = lax.all_gather(portion, "amp", axis=1, tiled=True).reshape(
        path_count * half_paths * 2, 2, rows_here
    )
    right = cut_term(right_slabs, mixes(term_index, right_terms))
    right = apply_low(right, right_gates[0])
    right_moved = lax.all_to_all(right, "amp", split_axis=0, concat_axis=2, tiled=True)
    right_turned = right_high(right_moved, right_gates[1])
    right = lax.all_to_all(right_turned, "amp", split_axis=2, concat_axis=0, tiled=True)
    everything = lax.all_gather(right, "path", axis=0, tiled=True)
    real_part, imag_part = contract(row_block, everything)
    return jnp.stack([real_part, imag_part], 0).astype(jnp.bfloat16)


def solution(mesh):
    return jax.shard_map(
        shards,
        mesh=mesh,
        in_specs=(
            P(("grp", "path"), None, "amp"),
            P(("grp", "path"), None, "amp"),
            P(("grp", "path")),
            P(),
            P(),
            P(),
            P(),
        ),
        out_specs=P(None, ("grp", "path"), "amp"),
        check_vma=False,
    )
```

profile of v0, /device:TPU:0, one launch (start us, length us, event | category | flops | bytes accessed | tf_op | source)
XLA Modules:
  0.0 288.8 jit_solution(7753225383539384605)
XLA Ops:
  7.3 0.8 slice_bitcast_fusion.20
  9.0 0.8 fusion.66
  9.8 1.4 reshape.234
  11.3 18.8 %broadcast_multiply_fusion.3 = (f32[16,2,2,64,64]{0,1,4,2,3:T(2,128)}, f32[16,2,2,64,64]{0,1,4,2,3:T(2,128)}, f32[16,2,2,64,64]{0,1,4,2,3:T(2,128)}, f32[16,2,2,64,64]{0,1,4,2,3:T(2,128)}) fusion(f32[64,64]{1,0:T(8,128)S(1)} %fusion.61, f32[16,2,2]{0,1,2:T(2,128)S(1)} %copy.56, f32[16,2,2]{0,1,2:T(2,128)S(1)} %copy.59, f32[16,2,2]{0,1,2:T(2,128)S(1)} %copy.69, ...), kind=kLoop, calls=%fused_computation.6 | loop fusion | flops 1048576 | bytes 4211712 | tf_op jit(solution)/shard_map/ab,nmj->najbm/dot_general | solution.py:14
  30.1 5.2 %copy.58 = f32[16,128,128]{2,1,0:T(8,128)S(1)} copy(f32[16,128,128]{0,2,1:T(8,128)} %bitcast.165) | data formatting | bytes 2097152 | tf_op jit(solution)/shard_map/reshape | solution.py:14
  35.3 5.2 %copy.60 = f32[16,128,128]{2,1,0:T(8,128)S(1)} copy(f32[16,128,128]{0,2,1:T(8,128)} %bitcast.164) | data formatting | bytes 2097152 | tf_op jit(solution)/shard_map/reshape | solution.py:14
  43.8 2.0 pad_maximum_fusion.4
  45.8 3.7 %all-to-all-start = ((bf16[16,2,8192]{2,1,0:T(2,128)(2,1)}), bf16[16,2,8192]{2,1,0:T(2,128)(2,1)S(1)}, u32[]{:S(2)}, u32[]{:S(2)}) async-start(bf16[16,2,8192]{2,1,0:T(2,128)(2,1)} %pad_maximum_fusion.4), calls=%async_computation | async-start | bytes 1048576 | tf_op jit(solution)/shard_map/all_to_all | solution.py:118
  50.5 10.0 %reshape_squeeze.17 = bf16[2,64,2,64,2]{4,3,2,1,0:T(8,128)(2,1)} reshape(bf16[1,2,128,128]{3,2,1,0:T(8,128)(2,1)S(1)} %slice-done) | data formatting | bytes 131072 | tf_op jit(solution)/shard_map/reshape;squeeze | solution.py:70
  60.5 7.9 %slice_reduce_fusion = (bf16[64,64]{1,0:T(8,128)(2,1)S(1)}, bf16[64,64]{1,0:T(8,128)(2,1)S(1)}, bf16[64,64]{1,0:T(8,128)(2,1)S(1)}, bf16[64,64]{1,0:T(8,128)(2,1...) fusion(bf16[2,64,2,64,2]{4,3,2,1,0:T(8,128)(2,1)} %reshape_sque, ...), kind=kLoop, calls=%fused_computation.34 | loop fusion | bytes 131072 | tf_op jit(solution)/shard_map/slice | solution.py:53
  68.5 5.2 %copy.71 = f32[16,128,128]{2,1,0:T(8,128)S(1)} copy(f32[16,128,128]{0,2,1:T(8,128)} %bitcast.163) | data formatting | bytes 2097152 | tf_op jit(solution)/shard_map/reshape | solution.py:14
  73.8 5.2 %copy.73 = f32[16,128,128]{2,1,0:T(8,128)S(1)} copy(f32[16,128,128]{0,2,1:T(8,128)} %bitcast.162) | data formatting | bytes 2097152 | tf_op jit(solution)/shard_map/reshape | solution.py:14
  81.9 1.3 pad_maximum_fusion.5
  83.2 3.4 %all-to-all-start.2 = ((bf16[16,2,4096]{2,1,0:T(2,128)(2,1)}), bf16[16,2,4096]{2,1,0:T(2,128)(2,1)S(1)}, u32[]{:S(2)}, u32[]{:S(2)}) async-start(bf16[16,2,4096]{2,1,0:T(2,128)(2,1)} %pad_maximum_fusion.5), calls=%async_computation.2 | async-start | bytes 524288 | tf_op jit(solution)/shard_map/all_to_all | solution.py:134
  88.2 12.8 %copy.66 = bf16[8,2,16384]{0,1,2:T(2,128)(2,1)} copy(bf16[8,2,16384]{2,1,0:T(2,128)(2,1)S(1)} %reshape.222) | data formatting | bytes 1048576 | tf_op jit(solution)/shard_map/reshape | solution.py:125
  100.9 11.1 %reshape.246 = bf16[8,2,16384]{2,1,0:T(2,128)(2,1)} reshape(bf16[16384,2,8]{2,1,0:T(2,128)(2,1)} %bitcast.160) | data formatting | bytes 1048576
  112.1 7.3 %all-to-all-start.1 = ((bf16[8,2,16384]{2,1,0:T(2,128)(2,1)}), bf16[8,2,16384]{2,1,0:T(2,128)(2,1)S(1)}, u32[]{:S(2)}, u32[]{:S(2)}) async-start(bf16[8,2,16384]{2,1,0:T(2,128)(2,1)} %reshape.246), calls=%async_computation.1 | async-start | bytes 1048576 | tf_op jit(solution)/shard_map/all_to_all | solution.py:126
  121.6 12.9 %all-to-all-done.1 = bf16[8,2,16384]{2,1,0:T(2,128)(2,1)S(1)} async-done(((bf16[8,2,16384]{2,1,0:T(2,128)(2,1)}), bf16[8,2,16384]{2,1,0:T(2,128)(2,1)S(1)}, u32[]{:S(2)}, u32[]{:S(2)}) %all-to-all-start.1) | async-done | bytes 524320 | tf_op jit(solution)/shard_map/all_to_all | solution.py:126
  134.5 10.9 %reshape.247 = bf16[16384,2,8]{2,1,0:T(2,128)(2,1)} reshape(bf16[8,2,16384]{2,1,0:T(2,128)(2,1)S(1)} %all-to-all-done.1) | data formatting | bytes 1048576
  145.4 12.5 %copy.85 = bf16[8,2,8,2048]{3,2,0,1:T(8,128)(2,1)} copy(bf16[8,2,8,2048]{0,1,3,2:T(2,128)(2,1)} %bitcast.161) | data formatting | bytes 1048576 | tf_op jit(solution)/shard_map/all_to_all | solution.py:126
  159.1 6.8 %copy.80 = bf16[8,2,8192]{0,1,2:T(2,128)(2,1)} copy(bf16[8,2,8192]{2,1,0:T(2,128)(2,1)S(1)} %reshape.232) | data formatting | bytes 524288 | tf_op jit(solution)/shard_map/reshape | solution.py:88
  165.9 6.1 %reshape.244 = bf16[2,2,32768]{2,1,0:T(2,128)(2,1)S(1)} reshape(bf16[8192,2,8]{2,1,0:T(2,128)(2,1)} %bitcast.166) | data formatting | bytes 524288
  172.0 3.9 %all_to_all.63 = bf16[2,2,32768]{2,1,0:T(2,128)(2,1)S(1)} all-to-all(bf16[2,2,32768]{2,1,0:T(2,128)(2,1)S(1)} %reshape.244), channel_id=1, replica_groups=mesh['grp'=2,'path'=8,'amp'=2] {'amp'}, dimensions={0} | all-to-all | bytes 524288 | tf_op jit(solution)/shard_map/all_to_all | solution.py:136
  175.9 6.2 %reshape.245 = bf16[8192,2,8]{2,1,0:T(2,128)(2,1)} reshape(bf16[2,2,32768]{2,1,0:T(2,128)(2,1)S(1)} %all_to_all.63) | data formatting | bytes 524288
  182.1 9.3 %copy.82 = bf16[2,8,2,4096]{3,1,0,2:T(8,128)(2,1)} copy(bf16[2,8,2,4096]{1,2,3,0:T(2,128)(2,1)} %bitcast.167) | data formatting | bytes 524288 | tf_op jit(solution)/shard_map/all_to_all | solution.py:136
  191.4 1.8 copy.68
  193.4 46.4 %all-gather.5.cloned.1.call-done = bf16[128,2,4096]{2,0,1:T(8,128)(2,1)} async-done(((bf16[16,2,4096]{2,0,1:T(8,128)(2,1)}), bf16[128,2,4096]{2,0,1:T(8,128)(2,1)}) %all-gather.5.cloned.1.call-update) | async-done | bytes 2097168 | tf_op jit(solution)/shard_map/all_gather | solution.py:137
  239.8 1.7 slice_bitcast_fusion
  241.5 8.1 %convert_bitcast_fusion = bf16[1,2048,4096]{2,1,0:T(8,128)(2,1)} fusion(bf16[128,4096]{1,0:T(8,128)(2,1)S(1)} %get-tuple-element.14, bf16[128,4096]{1,0:T(8,128)(2,1)S(1)} %get-tuple-element.13, bf16[128,2048]{1,0:T(8,128)(2,1)S(1)} %get-tuple-element.16, bf16[128,2048]{1,0:T(8,128)(2,1)S(1)} %get-tuple-element.15), kind=kOutput, calls=%fused_computation.1 | convolution fusion | flops 4309647360 | bytes 19922944 | tf_op jit(solution)/shard_map/dot_general | solution.py:99
  249.6 1.3 fusion.82
  250.9 8.1 %convert_bitcast_fusion.1 = bf16[1,2048,4096]{2,1,0:T(8,128)(2,1)} fusion(bf16[128,4096]{1,0:T(8,128)(2,1)S(1)} %fusion.82, bf16[128,4096]{1,0:T(8,128)(2,1)S(1)} %get-tuple-element.14, bf16[128,2048]{1,0:T(8,128)(2,1)S(1)} %get-tuple-element.16, bf16[128,2048]{1,0:T(8,128)(2,1)S(1)} %get-tuple-element.15), kind=kOutput, calls=%fused_computation.2 | convolution fusion | flops 4309647360 | bytes 19922944 | tf_op jit(solution)/shard_map/dot_general | solution.py:96
  259.0 23.0 %pad_maximum_fusion = bf16[2,2048,4096]{2,1,0:T(8,128)(2,1)} fusion(bf16[1,2048,4096]{2,1,0:T(8,128)(2,1)} %convert_bitcast_fusion, bf16[1,2048,4096]{2,1,0:T(8,128)(2,1)} %convert_bitcast_fusion.1), kind=kLoop, calls=%fused_computation | loop fusion | flops 16777216 | bytes 67108864 | tf_op jit(solution)/shard_map/stack | solution.py:139
  (72 shorter events, 13.5 us)
Async XLA Ops:
  6.5 1.6 copy-start
  40.6 9.7 %copy-start.2 = (bf16[2,2,128,128]{3,2,1,0:T(8,128)(2,1)S(1)}, bf16[2,2,128,128]{3,2,1,0:T(8,128)(2,1)}, u32[]{:S(2)}) copy-start(bf16[2,2,128,128]{3,2,1,0:T(8,128)(2,1)} %param.13) | copy-start | bytes 393220
  40.6 9.7 %copy-start.3 = (bf16[16,2,4096]{2,1,0:T(2,128)(2,1)S(1)}, bf16[16,2,4096]{2,1,0:T(2,128)(2,1)}, u32[]{:S(2)}) copy-start(bf16[16,2,4096]{2,1,0:T(2,128)(2,1)} %param.8) | copy-start | bytes 786436
  40.6 9.9 %slice-start = ((bf16[2,2,128,128]{3,2,1,0:T(8,128)(2,1)}), bf16[1,2,128,128]{3,2,1,0:T(8,128)(2,1)S(1)}, s32[]{:S(2)}) async-start(bf16[2,2,128,128]{3,2,1,0:T(8,128)(2,1)} %param.13), calls=%async_computation.6 | async-start | bytes 131072 | tf_op jit(solution)/shard_map/slice | solution.py:135
  45.8 37.4 %all-to-all-start = ((bf16[16,2,8192]{2,1,0:T(2,128)(2,1)}), bf16[16,2,8192]{2,1,0:T(2,128)(2,1)S(1)}, u32[]{:S(2)}, u32[]{:S(2)}) async-start(bf16[16,2,8192]{2,1,0:T(2,128)(2,1)} %pad_maximum_fusion.4), calls=%async_computation | async-start | bytes 1048576 | tf_op jit(solution)/shard_map/all_to_all | solution.py:118
  83.2 28.9 %all-to-all-start.2 = ((bf16[16,2,4096]{2,1,0:T(2,128)(2,1)}), bf16[16,2,4096]{2,1,0:T(2,128)(2,1)S(1)}, u32[]{:S(2)}, u32[]{:S(2)}) async-start(bf16[16,2,4096]{2,1,0:T(2,128)(2,1)} %pad_maximum_fusion.5), calls=%async_computation.2 | async-start | bytes 524288 | tf_op jit(solution)/shard_map/all_to_all | solution.py:134
  112.1 22.5 %all-to-all-start.1 = ((bf16[8,2,16384]{2,1,0:T(2,128)(2,1)}), bf16[8,2,16384]{2,1,0:T(2,128)(2,1)S(1)}, u32[]{:S(2)}, u32[]{:S(2)}) async-start(bf16[8,2,16384]{2,1,0:T(2,128)(2,1)} %reshape.246), calls=%async_computation.1 | async-start | bytes 1048576 | tf_op jit(solution)/shard_map/all_to_all | solution.py:126
  119.4 72.0 %all-gather.3.cloned.1.call-start = ((), (), s32[]{:S(2)}) async-start(), calls=%async_computation.4 | async-start | bytes 1572864 | tf_op jit(solution)/shard_map/all_gather | solution.py:129
  158.0 81.8 %all-gather.5.cloned.1.call-start = ((), (), s32[]{:S(2)}) async-start(), calls=%async_computation.5 | async-start | bytes 2359296 | tf_op jit(solution)/shard_map/all_gather | solution.py:137
  259.0 23.0 %copy-start.1 = (f32[4,2,2,2]{0,3,2,1:T(2,128)S(1)}, f32[4,2,2,2]{0,3,2,1:T(2,128)}, u32[]{:S(2)}) copy-start(f32[4,2,2,2]{0,3,2,1:T(2,128)} %param.10) | copy-start | bytes 388
Sparse Core Ops, SparseCore 0:
  158.1 8.0 all-gather.2
  191.5 48.2 all-gather.4
where the time goes:
time: 290 us; the launch traced here: 289 us
  local copies, waits for them, and re-layouts  123 us (42%)
  waiting for transfers between devices  59.4 us (20%)
  other arithmetic  48.2 us (17%)
  matrix products  25.9 us (9%)
  starting transfers between devices  14.7 us (5%)
  between operations  13.9 us (5%)
  blocking collectives  3.94 us (1%)
    all_gather x1, waiting for transfers between devices, shards(): everything = lax.all_gather(right, 'path', axis=0, tiled=True)  46.4 us
    unnamed x12, local copies, waits for them, and re-layouts  34.3 us
    another operation x1, other arithmetic, shards(): return jnp.stack([real_part, imag_part], 0).astype(jnp.bfloat16)  23 us
    reshape x4, local copies, waits for them, and re-layouts, expand(): jnp.einsum('ab,nmj->najbm', identity, part)  20.9 us
    dot_general x1, other arithmetic, expand(): jnp.einsum('ab,nmj->najbm', identity, part)  18.8 us
    reshape x2, local copies, waits for them, and re-layouts, shards(): turned = turned.astype(jnp.bfloat16).reshape(half_paths, 2, full_left)  12.9 us
    all_to_all x1, waiting for transfers between devices, shards(): lax.all_to_all(turned, 'path', split_axis=2, concat_axis=0, tiled=True)  12.9 us
    all_to_all x1, local copies, waits for them, and re-layouts, shards(): lax.all_to_all(turned, 'path', split_axis=2, concat_axis=0, tiled=True)  12.5 us
  transfers between devices with their start and end apart: 5, of which 2 were waited for; matrix products, arithmetic and copies ran while one was open for 32% of the time, Pallas kernels for 0%

commit v1 on v0

--- a/solution.py
+++ b/solution.py
@@ -134,7 +134,12 @@
     right_moved = lax.all_to_all(right, "amp", split_axis=0, concat_axis=2, tiled=True)
     right_turned = right_high(right_moved, right_gates[1])
     right = lax.all_to_all(right_turned, "amp", split_axis=2, concat_axis=0, tiled=True)
-    everything = lax.all_gather(right, "path", axis=0, tiled=True)
+    ring = [right]
+    for hop in range(7):
+        ring.append(lax.ppermute(ring[-1], "path", [(dev, (dev + 1) % 8) for dev in range(8)]))
+    everything = jnp.roll(
+        jnp.concatenate(ring[::-1], axis=0), (lax.axis_index("path") + 1) * ring[0].shape[0], axis=0
+    )
     real_part, imag_part = contract(row_block, everything)
     return jnp.stack([real_part, imag_part], 0).astype(jnp.bfloat16)
 

time: 290 us -> 283 us (0.976)
  waiting for transfers between devices: 59.4 us -> 46.5 us
  blocking collectives: 3.94 us -> 8.1 us
    all_gather x1 -> x0, waiting for transfers between devices: 46.4 us -> none  [shards(): everything = lax.all_gather(right, 'path', axis=0, tiled=True)]
    ppermute x0 -> x7, waiting for transfers between devices: none -> 36.2 us  [shards(): lax.ppermute(ring[-1], 'path', [(dev, (dev + 1) % 8) for dev in range(8)])]
    all_to_all x1, waiting for transfers between devices: 12.9 us -> 0.01 us  [shards(): lax.all_to_all(turned, 'path', split_axis=2, concat_axis=0, tiled=True)]
    all_gather x1, waiting for transfers between devices: 0.02 us -> 8.84 us  [shards(): lax.all_gather(portion, 'amp', axis=1, tiled=True)]
    ppermute x0 -> x7, starting transfers between devices: none -> 6.71 us  [shards(): lax.ppermute(ring[-1], 'path', [(dev, (dev + 1) % 8) for dev in range(8)])]
    all_to_all x0 -> x1, blocking collectives: none -> 4.15 us  [shards(): moved = lax.all_to_all(left, 'amp', split_axis=0, concat_axis=2, tiled=True)]
    all_to_all x1 -> x0, starting transfers between devices: 3.67 us -> none  [shards(): moved = lax.all_to_all(left, 'amp', split_axis=0, concat_axis=2, tiled=True)]
    unnamed x12 -> x33, local copies, waits for them, and re-layouts: 34.3 us -> 34.6 us
  transfers between devices with their start and end apart: 5 -> 10, of which waited for: 2 -> 6; matrix products, arithmetic and copies ran while one was open for 32% -> 24% of each run, Pallas kernels for 0% -> 0%
where the time goes in v1:
time: 283 us; the launch traced here: 281 us
  local copies, waits for them, and re-layouts  121 us (43%)
  other arithmetic  48 us (17%)
  waiting for transfers between devices  46.5 us (16%)
  matrix products  27.2 us (10%)
  starting transfers between devices  16.4 us (6%)
  between operations  14 us (5%)
  blocking collectives  8.1 us (3%)
    ppermute x7, waiting for transfers between devices, shards(): lax.ppermute(ring[-1], 'path', [(dev, (dev + 1) % 8) for dev in range(8)])  36.2 us
    unnamed x33, local copies, waits for them, and re-layouts  34.6 us
    another operation x1, other arithmetic, shards(): return jnp.stack([real_part, imag_part], 0).astype(jnp.bfloat16)  23 us
    reshape x4, local copies, waits for them, and re-layouts, expand(): jnp.einsum('ab,nmj->najbm', identity, part)  20.9 us
    dot_general x1, other arithmetic, expand(): jnp.einsum('ab,nmj->najbm', identity, part)  18.9 us
    reshape x2, local copies, waits for them, and re-layouts, shards(): turned = turned.astype(jnp.bfloat16).reshape(half_paths, 2, full_left)  12.9 us
    all_to_all x1, local copies, waits for them, and re-layouts, shards(): lax.all_to_all(turned, 'path', split_axis=2, concat_axis=0, tiled=True)  12.5 us
    another operation x1, local copies, waits for them, and re-layouts, right_high(): blocks = gate_mat.reshape(2, low_width, 2, low_width, 2)  10 us
  transfers between devices with their start and end apart: 10, of which 6 were waited for; matrix products, arithmetic and copies ran while one was open for 24% of the time, Pallas kernels for 0%

profile of v1, /device:TPU:0, one launch (start us, length us, event | category | flops | bytes accessed | tf_op | source)
XLA Modules:
  0.0 281.5 jit_solution(17611602408648120674)
XLA Ops:
  10.9 18.9 %broadcast_multiply_fusion.3 = (f32[16,2,2,64,64]{0,1,4,2,3:T(2,128)}, f32[16,2,2,64,64]{0,1,4,2,3:T(2,128)}, f32[16,2,2,64,64]{0,1,4,2,3:T(2,128)}, f32[16,2,2,64,64]{0,1,4,2,3:T(2,128)}) fusion(f32[64,64]{1,0:T(8,128)S(1)} %fusion.61, f32[16,2,2]{0,1,2:T(2,128)S(1)} %copy.56, f32[16,2,2]{0,1,2:T(2,128)S(1)} %copy.59, f32[16,2,2]{0,1,2:T(2,128)S(1)} %copy.69, ...), kind=kLoop, calls=%fused_computation.6 | loop fusion | flops 1048576 | bytes 4211712 | tf_op jit(solution)/shard_map/ab,nmj->najbm/dot_general | solution.py:14
  29.8 5.2 %copy.71 = f32[16,128,128]{2,1,0:T(8,128)S(1)} copy(f32[16,128,128]{0,2,1:T(8,128)} %bitcast.166) | data formatting | bytes 2097152 | tf_op jit(solution)/shard_map/reshape | solution.py:14
  35.0 5.2 %copy.73 = f32[16,128,128]{2,1,0:T(8,128)S(1)} copy(f32[16,128,128]{0,2,1:T(8,128)} %bitcast.165) | data formatting | bytes 2097152 | tf_op jit(solution)/shard_map/reshape | solution.py:14
  44.5 3.6 %all-to-all-start.2 = ((bf16[16,2,4096]{2,1,0:T(2,128)(2,1)}), bf16[16,2,4096]{2,1,0:T(2,128)(2,1)S(1)}, u32[]{:S(2)}, u32[]{:S(2)}) async-start(bf16[16,2,4096]{2,1,0:T(2,128)(2,1)} %pad_maximum_fusion.5), calls=%async_computation.2 | async-start | bytes 524288 | tf_op jit(solution)/shard_map/all_to_all | solution.py:134
  48.1 1.5 all-to-all-done.2
  51.5 10.0 %reshape_squeeze.17 = bf16[2,64,2,64,2]{4,3,2,1,0:T(8,128)(2,1)} reshape(bf16[1,2,128,128]{3,2,1,0:T(8,128)(2,1)S(1)} %slice-done) | data formatting | bytes 131072 | tf_op jit(solution)/shard_map/reshape;squeeze | solution.py:70
  61.6 8.1 %slice_reduce_fusion = (bf16[64,64]{1,0:T(8,128)(2,1)S(1)}, bf16[64,64]{1,0:T(8,128)(2,1)S(1)}, bf16[64,64]{1,0:T(8,128)(2,1)S(1)}, bf16[64,64]{1,0:T(8,128)(2,1...) fusion(bf16[2,64,2,64,2]{4,3,2,1,0:T(8,128)(2,1)} %reshape_sque, ...), kind=kLoop, calls=%fused_computation.34 | loop fusion | bytes 131072 | tf_op jit(solution)/shard_map/slice | solution.py:53
  70.8 6.8 %copy.80 = bf16[8,2,8192]{0,1,2:T(2,128)(2,1)} copy(bf16[8,2,8192]{2,1,0:T(2,128)(2,1)S(1)} %reshape.232) | data formatting | bytes 524288 | tf_op jit(solution)/shard_map/reshape | solution.py:88
  77.7 6.1 %reshape.244 = bf16[2,2,32768]{2,1,0:T(2,128)(2,1)S(1)} reshape(bf16[8192,2,8]{2,1,0:T(2,128)(2,1)} %bitcast.167) | data formatting | bytes 524288
  83.8 3.9 %all_to_all.63 = bf16[2,2,32768]{2,1,0:T(2,128)(2,1)S(1)} all-to-all(bf16[2,2,32768]{2,1,0:T(2,128)(2,1)S(1)} %reshape.244), channel_id=1, replica_groups=mesh['grp'=2,'path'=8,'amp'=2] {'amp'}, dimensions={0} | all-to-all | bytes 524288 | tf_op jit(solution)/shard_map/all_to_all | solution.py:136
  87.7 6.2 %reshape.245 = bf16[8192,2,8]{2,1,0:T(2,128)(2,1)} reshape(bf16[2,2,32768]{2,1,0:T(2,128)(2,1)S(1)} %all_to_all.63) | data formatting | bytes 524288
  93.9 8.2 %copy.82 = bf16[2,8,2,4096]{3,1,0,2:T(8,128)(2,1)S(1)} copy(bf16[2,8,2,4096]{1,2,3,0:T(2,128)(2,1)} %bitcast.168) | data formatting | bytes 524288 | tf_op jit(solution)/shard_map/all_to_all | solution.py:136
  102.1 3.1 %collective-permute-start = (bf16[16,2,4096]{2,0,1:T(8,128)(2,1)S(1)}, bf16[16,2,4096]{2,0,1:T(8,128)(2,1)S(1)}, u32[]{:S(2)}, u32[]{:S(2)}) collective-permute-start(bf16[16,2,4096]{2,0,1:T(8,128)(2,1)S(1)} %bitcast.170), channel_id=1, source_target_pairs={{0,2},{2,4},{4,6},{6,8},{8,10},{10,12},{12,14},{14,0},{1,3},{3,5},... | collective-permute-start | bytes 786440 | tf_op jit(solution)/shard_map/ppermute | solution.py:139
  106.9 5.2 %copy.58 = f32[16,128,128]{2,1,0:T(8,128)S(1)} copy(f32[16,128,128]{0,2,1:T(8,128)} %bitcast.164) | data formatting | bytes 2097152 | tf_op jit(solution)/shard_map/reshape | solution.py:14
  112.2 5.2 %copy.60 = f32[16,128,128]{2,1,0:T(8,128)S(1)} copy(f32[16,128,128]{0,2,1:T(8,128)} %bitcast.163) | data formatting | bytes 2097152 | tf_op jit(solution)/shard_map/reshape | solution.py:14
  120.7 1.6 collective-permute-start.1
  123.4 4.2 %all_to_all.64 = bf16[16,2,8192]{2,1,0:T(2,128)(2,1)S(1)} all-to-all(bf16[16,2,8192]{2,1,0:T(2,128)(2,1)S(1)} %pad_maximum_fusion.4), channel_id=1, replica_groups=mesh['grp'=2,'path'=8,'amp'=2] {'amp'}, dimensions={0} | all-to-all | bytes 1048576 | tf_op jit(solution)/shard_map/all_to_all | solution.py:118
  128.5 3.0 %collective-permute-done.1 = bf16[16,2,4096]{2,0,1:T(8,128)(2,1)S(1)} collective-permute-done((bf16[16,2,4096]{2,0,1:T(8,128)(2,1)S(1)}, bf16[16,2,4096]{2,0,1:T(8,128)(2,1)S(1)}, u32[]{:S(2)}, u32[]{:S(2)}) %collective-permute-start.1) | collective-permute-done | bytes 262176 | tf_op jit(solution)/shard_map/ppermute | solution.py:139
  132.4 9.0 %collective-permute-done.2 = bf16[16,2,4096]{2,0,1:T(8,128)(2,1)S(1)} collective-permute-done((bf16[16,2,4096]{2,0,1:T(8,128)(2,1)S(1)}, bf16[16,2,4096]{2,0,1:T(8,128)(2,1)S(1)}, u32[]{:S(2)}, u32[]{:S(2)}) %collective-permute-start.2) | collective-permute-done | bytes 262176 | tf_op jit(solution)/shard_map/ppermute | solution.py:139
  142.0 12.8 %copy.66 = bf16[8,2,16384]{0,1,2:T(2,128)(2,1)} copy(bf16[8,2,16384]{2,1,0:T(2,128)(2,1)S(1)} %reshape.222) | data formatting | bytes 1048576 | tf_op jit(solution)/shard_map/reshape | solution.py:125
  154.8 11.1 %reshape.246 = bf16[8,2,16384]{2,1,0:T(2,128)(2,1)} reshape(bf16[16384,2,8]{2,1,0:T(2,128)(2,1)} %bitcast.161) | data formatting | bytes 1048576
  165.9 6.0 %all-to-all-start.1 = ((bf16[8,2,16384]{2,1,0:T(2,128)(2,1)}), bf16[8,2,16384]{2,1,0:T(2,128)(2,1)S(1)}, u32[]{:S(2)}, u32[]{:S(2)}) async-start(bf16[8,2,16384]{2,1,0:T(2,128)(2,1)} %reshape.246), calls=%async_computation.1 | async-start | bytes 1048576 | tf_op jit(solution)/shard_map/all_to_all | solution.py:126
  171.9 2.0 collective-permute-start.4
  174.0 15.1 %collective-permute-done.4 = bf16[16,2,4096]{2,0,1:T(8,128)(2,1)S(1)} collective-permute-done((bf16[16,2,4096]{2,0,1:T(8,128)(2,1)S(1)}, bf16[16,2,4096]{2,0,1:T(8,128)(2,1)S(1)}, u32[]{:S(2)}, u32[]{:S(2)}) %collective-permute-start.4) | collective-permute-done | bytes 262176 | tf_op jit(solution)/shard_map/ppermute | solution.py:139
  189.1 9.1 %collective-permute-done.5 = bf16[16,2,4096]{2,0,1:T(8,128)(2,1)S(1)} collective-permute-done((bf16[16,2,4096]{2,0,1:T(8,128)(2,1)S(1)}, bf16[16,2,4096]{2,0,1:T(8,128)(2,1)S(1)}, u32[]{:S(2)}, u32[]{:S(2)}) %collective-permute-start.5) | collective-permute-done | bytes 262176 | tf_op jit(solution)/shard_map/ppermute | solution.py:139
  198.1 10.9 %reshape.247 = bf16[16384,2,8]{2,1,0:T(2,128)(2,1)} reshape(bf16[8,2,16384]{2,1,0:T(2,128)(2,1)S(1)} %all-to-all-done.1) | data formatting | bytes 1048576
  209.0 12.5 %copy.85 = bf16[8,2,8,2048]{3,2,0,1:T(8,128)(2,1)} copy(bf16[8,2,8,2048]{0,1,3,2:T(2,128)(2,1)} %bitcast.162) | data formatting | bytes 1048576 | tf_op jit(solution)/shard_map/all_to_all | solution.py:126
  223.3 8.8 %all-gather.2.cloned.1.call-done = bf16[8,16,2,2048]{3,0,1,2:T(8,128)(2,1)} async-done(((bf16[8,8,2,2048]{3,0,1,2:T(8,128)(2,1)}), bf16[8,16,2,2048]{3,0,1,2:T(8,128)(2,1)}) %all-gather.2.cloned.1.call-update) | async-done | bytes 1048592 | tf_op jit(solution)/shard_map/all_gather | solution.py:129
  232.1 1.8 copy.68
  234.1 9.4 %convert_bitcast_fusion = bf16[1,2048,4096]{2,1,0:T(8,128)(2,1)} fusion(bf16[128,4096]{1,0:T(8,128)(2,1)S(1)} %dynamic-slice_bitcast_fusion.1, bf16[128,4096]{1,0:T(8,128)(2,1)} %get-tuple-element.14, bf16[128,2048]{1,0:T(8,128)(2,1)S(1)} %get-tuple-element.16, bf16[128,2048]{1,0:T(8,128)(2,1)S(1)} %get-tuple-element.15), kind=kOutput, calls=%fused_computation.1 | convolution fusion | flops 4309647360 | bytes 19922944 | tf_op jit(solution)/shard_map/dot_general | solution.py:99
  243.4 8.2 %convert_bitcast_fusion.1 = bf16[1,2048,4096]{2,1,0:T(8,128)(2,1)} fusion(bf16[128,4096]{1,0:T(8,128)(2,1)S(1)} %get-tuple-element.13, bf16[128,4096]{1,0:T(8,128)(2,1)S(1)} %dynamic-slice_bitcast_fusion.1, bf16[128,2048]{1,0:T(8,128)(2,1)S(1)} %get-tuple-element.16, bf16[128,2048]{1,0:T(8,128)(2,1)S(1)} %get-tuple-element.15), kind=kOutput, calls=%fused_computation.2 | convolution fusion | flops 4309647360 | bytes 19922944 | tf_op jit(solution)/shard_map/dot_general | solution.py:96
  251.6 23.0 %pad_maximum_fusion = bf16[2,2048,4096]{2,1,0:T(8,128)(2,1)} fusion(bf16[1,2048,4096]{2,1,0:T(8,128)(2,1)} %convert_bitcast_fusion, bf16[1,2048,4096]{2,1,0:T(8,128)(2,1)} %convert_bitcast_fusion.1), kind=kLoop, calls=%fused_computation | loop fusion | flops 16777216 | bytes 67108864 | tf_op jit(solution)/shard_map/stack | solution.py:144
  (104 shorter events, 21.6 us)
Async XLA Ops:
  6.5 1.6 copy-start
  42.1 9.4 %slice-start = ((bf16[2,2,128,128]{3,2,1,0:T(8,128)(2,1)}), bf16[1,2,128,128]{3,2,1,0:T(8,128)(2,1)S(1)}, s32[]{:S(2)}) async-start(bf16[2,2,128,128]{3,2,1,0:T(8,128)(2,1)} %param.13), calls=%async_computation.5 | async-start | bytes 131072 | tf_op jit(solution)/shard_map/slice | solution.py:135
  44.5 5.2 %all-to-all-start.2 = ((bf16[16,2,4096]{2,1,0:T(2,128)(2,1)}), bf16[16,2,4096]{2,1,0:T(2,128)(2,1)S(1)}, u32[]{:S(2)}, u32[]{:S(2)}) async-start(bf16[16,2,4096]{2,1,0:T(2,128)(2,1)} %pad_maximum_fusion.5), calls=%async_computation.2 | async-start | bytes 524288 | tf_op jit(solution)/shard_map/all_to_all | solution.py:134
  87.7 17.5 %copy-start.3 = (bf16[2,2,128,128]{3,2,1,0:T(8,128)(2,1)S(1)}, bf16[2,2,128,128]{3,2,1,0:T(8,128)(2,1)}, u32[]{:S(2)}) copy-start(bf16[2,2,128,128]{3,2,1,0:T(8,128)(2,1)} %param.12) | copy-start | bytes 393220
  87.7 18.8 %copy-start.2 = (bf16[16,2,8192]{2,1,0:T(2,128)(2,1)S(1)}, bf16[16,2,8192]{2,1,0:T(2,128)(2,1)}, u32[]{:S(2)}) copy-start(bf16[16,2,8192]{2,1,0:T(2,128)(2,1)} %param.7) | copy-start | bytes 1572868
  102.1 18.5 %collective-permute-start = (bf16[16,2,4096]{2,0,1:T(8,128)(2,1)S(1)}, bf16[16,2,4096]{2,0,1:T(8,128)(2,1)S(1)}, u32[]{:S(2)}, u32[]{:S(2)}) collective-permute-start(bf16[16,2,4096]{2,0,1:T(8,128)(2,1)S(1)} %bitcast.170), channel_id=1, source_target_pairs={{0,2},{2,4},{4,6},{6,8},{8,10},{10,12},{12,14},{14,0},{1,3},{3,5},... | collective-permute-start | bytes 786440 | tf_op jit(solution)/shard_map/ppermute | solution.py:139
  117.4 2.6 copy-start.4
  117.4 2.6 copy-start.5
  117.4 2.6 copy-start.6
  120.7 10.8 %collective-permute-start.1 = (bf16[16,2,4096]{2,0,1:T(8,128)(2,1)S(1)}, bf16[16,2,4096]{2,0,1:T(8,128)(2,1)S(1)}, u32[]{:S(2)}, u32[]{:S(2)}) collective-permute-start(bf16[16,2,4096]{2,0,1:T(8,128)(2,1)S(1)} %collective-permute-done), channel_id=1, source_target_pairs={{0,2},{2,4},{4,6},{6,8},{8,10},{10,12},{12,14},{14,0},{1,3},{3,5},... | collective-permute-start | bytes 786440 | tf_op jit(solution)/shard_map/ppermute | solution.py:139
  131.5 9.9 %collective-permute-start.2 = (bf16[16,2,4096]{2,0,1:T(8,128)(2,1)S(1)}, bf16[16,2,4096]{2,0,1:T(8,128)(2,1)S(1)}, u32[]{:S(2)}, u32[]{:S(2)}) collective-permute-start(bf16[16,2,4096]{2,0,1:T(8,128)(2,1)S(1)} %collective-permute-done.1), channel_id=1, source_target_pairs={{0,2},{2,4},{4,6},{6,8},{8,10},{10,12},{12,14},{14,0},{1,3},{3,5},... | collective-permute-start | bytes 786440 | tf_op jit(solution)/shard_map/ppermute | solution.py:139
  141.4 30.5 %collective-permute-start.3 = (bf16[16,2,4096]{2,0,1:T(8,128)(2,1)S(1)}, bf16[16,2,4096]{2,0,1:T(8,128)(2,1)S(1)}, u32[]{:S(2)}, u32[]{:S(2)}) collective-permute-start(bf16[16,2,4096]{2,0,1:T(8,128)(2,1)S(1)} %collective-permute-done.2), channel_id=1, source_target_pairs={{0,2},{2,4},{4,6},{6,8},{8,10},{10,12},{12,14},{14,0},{1,3},{3,5},... | collective-permute-start | bytes 786440 | tf_op jit(solution)/shard_map/ppermute | solution.py:139
  165.9 32.2 %all-to-all-start.1 = ((bf16[8,2,16384]{2,1,0:T(2,128)(2,1)}), bf16[8,2,16384]{2,1,0:T(2,128)(2,1)S(1)}, u32[]{:S(2)}, u32[]{:S(2)}) async-start(bf16[8,2,16384]{2,1,0:T(2,128)(2,1)} %reshape.246), calls=%async_computation.1 | async-start | bytes 1048576 | tf_op jit(solution)/shard_map/all_to_all | solution.py:126
  171.9 60.3 %all-gather.2.cloned.1.call-start = ((), (), s32[]{:S(2)}) async-start(), calls=%async_computation.4 | async-start | bytes 1572864 | tf_op jit(solution)/shard_map/all_gather | solution.py:129
  171.9 17.1 %collective-permute-start.4 = (bf16[16,2,4096]{2,0,1:T(8,128)(2,1)S(1)}, bf16[16,2,4096]{2,0,1:T(8,128)(2,1)S(1)}, u32[]{:S(2)}, u32[]{:S(2)}) collective-permute-start(bf16[16,2,4096]{2,0,1:T(8,128)(2,1)S(1)} %collective-permute-done.3), channel_id=1, source_target_pairs={{0,2},{2,4},{4,6},{6,8},{8,10},{10,12},{12,14},{14,0},{1,3},{3,5},... | collective-permute-start | bytes 786440 | tf_op jit(solution)/shard_map/ppermute | solution.py:139
  189.1 9.1 %collective-permute-start.5 = (bf16[16,2,4096]{2,0,1:T(8,128)(2,1)S(1)}, bf16[16,2,4096]{2,0,1:T(8,128)(2,1)S(1)}, u32[]{:S(2)}, u32[]{:S(2)}) collective-permute-start(bf16[16,2,4096]{2,0,1:T(8,128)(2,1)S(1)} %collective-permute-done.4), channel_id=1, source_target_pairs={{0,2},{2,4},{4,6},{6,8},{8,10},{10,12},{12,14},{14,0},{1,3},{3,5},... | collective-permute-start | bytes 786440 | tf_op jit(solution)/shard_map/ppermute | solution.py:139
  198.1 23.5 %collective-permute-start.6 = (bf16[16,2,4096]{2,0,1:T(8,128)(2,1)S(1)}, bf16[16,2,4096]{2,0,1:T(8,128)(2,1)S(1)}, u32[]{:S(2)}, u32[]{:S(2)}) collective-permute-start(bf16[16,2,4096]{2,0,1:T(8,128)(2,1)S(1)} %collective-permute-done.5), channel_id=1, source_target_pairs={{0,2},{2,4},{4,6},{6,8},{8,10},{10,12},{12,14},{14,0},{1,3},{3,5},... | collective-permute-start | bytes 786440 | tf_op jit(solution)/shard_map/ppermute | solution.py:139
  251.6 23.0 %copy-start.1 = (f32[4,2,2,2]{0,3,2,1:T(2,128)S(1)}, f32[4,2,2,2]{0,3,2,1:T(2,128)}, u32[]{:S(2)}) copy-start(f32[4,2,2,2]{0,3,2,1:T(2,128)} %param.10) | copy-start | bytes 388
Sparse Core Ops, SparseCore 0:
  221.7 10.3 all-gather.1
